TPU v7x, 32 devices: a whole 2x2x4 slice. The times are simulated.
32 devices in a mesh: groups: 2 (over x), seq: 16 (over z, y, core).
Axes of the slice: x: 2, y: 2, z: 4, core: 2. Of those that a mesh axis runs over, the one named last changes fastest.
Arguments:
- query: bfloat16 [16, 4096], P('groups'), parts along dimension 0, may hold values from -12 to 12
- new_key: bfloat16 [16, 1024], P('groups'), parts along dimension 0, may hold values from -12 to 12
- new_value: bfloat16 [16, 1024], P('groups'), parts along dimension 0, may hold values from -12 to 12
- cache_keys: bfloat16 [16, 1024, 1024], P('groups', 'seq'), parts along dimension 0, may hold values from -6 to 6
- cache_values: bfloat16 [16, 1024, 1024], P('groups', 'seq'), parts along dimension 0, may hold values from -6 to 6
- cache_lengths: int32 [16], P('groups'), parts along dimension 0, may hold values from 512 to 1024
- residual_input: bfloat16 [16, 4096], P('groups'), parts along dimension 0, may hold values from -6 to 6
- w_out: bfloat16 [4096, 4096], P('seq'), may hold values from -0.09375 to 0.09375
- norm_gain: bfloat16 [4096], replicated, may hold values from 0.099609375 to 1.8984375
- w_router: bfloat16 [4096, 4], replicated, may hold values from -0.09375 to 0.09375
- w_gate: bfloat16 [4096, 28672], P(None, 'seq'), may hold values from -0.09375 to 0.09375
- w_up: bfloat16 [4096, 28672], P(None, 'seq'), may hold values from -0.09375 to 0.09375
- expert_down_weight: bfloat16 [28672, 4096], P('seq'), may hold values from -0.09375 to 0.09375
- expert_ids: int32 [16, 2], P('groups'), parts along dimension 0, may hold values from 0 to 3, all different within a row
Outputs:
- attn_proj: bfloat16 [16, 4096], P('groups', 'seq'), parts along dimension 0
- layer_out: bfloat16 [16, 4096], P('groups', 'seq'), parts along dimension 0
There are 2 independent parts, one for each index of `groups`. A program takes and returns all parts, laid end to end along the dimension named above; an argument that names none is the same for every part. Nothing has to cross between parts.
Inputs may be any that keep to these rules, and one draw needn't show every extreme that they name: Cache positions 0 to cache_lengths[b] - 1 of sequence b are live, the rest are not read; the new key and value are always live. `expert_ids`: the two experts of a token differ.
All inputs are finite; a program needn't handle non-finite values.
Results may differ from a plain program's by a relative error of at most 0.012.
Values sent between devices are 32-bit elements; how exact they have to be, the bound alone decides.
A program may use at most 128 MiB of HBM per device.

v0:
```python
import math
import jax
import jax.numpy as jnp
from jax import lax
from jax.sharding import PartitionSpec as P

HEADS = 32
KV_HEADS = 8
HEAD_DIM = 128
FF = 7168
masked_score = -1e30


def joined(value, axis, join):
    pieces = jax.tree.map(lambda part: lax.all_gather(part, axis), value)
    head = jax.tree.map(lambda part: part[0], pieces)
    tail = jax.tree.map(lambda part: part[1:], pieces)
    so_far, _ = lax.scan(lambda so_far, share: (join(so_far, share), None), head, tail)
    return so_far


def merge_partial_results(first, second):
    first_max, first_sum, first_num = first
    second_max, second_sum, second_num = second
    ceiling = jnp.maximum(first_max, second_max)
    first_scale = jnp.exp(first_max - ceiling)
    second_scale = jnp.exp(second_max - ceiling)
    merged_sum = first_sum * first_scale + second_sum * second_scale
    merged_num = first_num * first_scale[..., None] + second_num * second_scale[..., None]
    return (ceiling, merged_sum, merged_num)


def per_device(
    query,
    new_key,
    new_value,
    cache_keys,
    cache_values,
    cache_lengths,
    residual_input,
    w_out,
    norm_gain,
    w_router,
    w_gate,
    w_up,
    expert_down_weight,
    expert_ids,
):
    seq_count = query.shape[0]
    per_group = HEADS // KV_HEADS
    local_len = cache_keys.shape[1]
    device = lax.axis_index("seq")
    inv_scale = 1.0 / math.sqrt(HEAD_DIM)
    query_vectors = query.reshape(seq_count, KV_HEADS, per_group, HEAD_DIM)
    key_block = cache_keys.reshape(seq_count, local_len, KV_HEADS, HEAD_DIM)
    value_block = cache_values.reshape(seq_count, local_len, KV_HEADS, HEAD_DIM)
    scores = (
        jnp.einsum("bkgd,btkd->bkgt", query_vectors, key_block, preferred_element_type=jnp.float32)
        * inv_scale
    )
    positions = device * local_len + jnp.arange(local_len, dtype=jnp.int32)
    is_live = (positions[None, :] < cache_lengths[:, None])[:, None, None, :]
    scores = jnp.where(is_live, scores, masked_score)
    incoming_key_rows = new_key.reshape(seq_count, KV_HEADS, HEAD_DIM)
    incoming_token_score = (
        jnp.einsum(
            "oqes,oqs->oqe", query_vectors, incoming_key_rows, preferred_element_type=jnp.float32
        )
        * inv_scale
    )
    fresh_value = new_value.astype(jnp.float32).reshape(seq_count, KV_HEADS, 1, HEAD_DIM)
    feat_width = w_out.shape[0]
    feat_start = device * feat_width
    flat_shape = (seq_count, HEADS * HEAD_DIM)
    local_max = jnp.max(scores, axis=-1)
    weights = jnp.where(is_live, jnp.exp(scores - local_max[..., None]), 0.0)
    numerator = jnp.einsum(
        "bkgt,btkd->bkgd",
        weights.astype(jnp.bfloat16),
        value_block,
        preferred_element_type=jnp.float32,
    )
    merged_max, merged_sum, merged_num = joined(
        (local_max, jnp.sum(weights, axis=-1), numerator), "seq", merge_partial_results
    )
    ceiling = jnp.maximum(merged_max, incoming_token_score)
    old_scale = jnp.exp(merged_max - ceiling)
    fresh_weight = jnp.exp(incoming_token_score - ceiling)
    fresh_rounded = lax.optimization_barrier(fresh_weight.astype(jnp.bfloat16)).astype(jnp.float32)
    numerator = merged_num * old_scale[..., None] + fresh_rounded[..., None] * fresh_value
    denominator = merged_sum * old_scale + fresh_weight
    context = (numerator / denominator[..., None]).reshape(flat_shape)
    context_own = lax.dynamic_slice_in_dim(context, feat_start, feat_width, 1).astype(jnp.bfloat16)
    projected = lax.psum(jnp.dot(context_own, w_out, preferred_element_type=jnp.float32), "seq")
    out_width = projected.shape[1] // lax.axis_size("seq")
    out_start = device * out_width
    attn_proj = lax.dynamic_slice_in_dim(projected, out_start, out_width, 1).astype(jnp.bfloat16)
    stream = residual_input.astype(jnp.float32) + projected
    normed = (
        stream
        * lax.rsqrt(jnp.mean(stream * stream, axis=-1, keepdims=True) + 1e-05)
        * norm_gain.astype(jnp.float32)
    )
    normed = normed.astype(jnp.bfloat16)
    logits = jnp.dot(normed, w_router, preferred_element_type=jnp.float32)
    expert_count = w_router.shape[1]
    picks = expert_ids[:, :, None] == jnp.arange(expert_count, dtype=jnp.int32)[None, None, :]
    chosen = jnp.sum(jnp.where(picks, logits[:, None, :], 0.0), axis=-1)
    first_gate = jax.nn.sigmoid(chosen[:, 0] - chosen[:, 1])
    gate_pair = jnp.stack([first_gate, 1.0 - first_gate], axis=1)
    own_expert = device * w_gate.shape[1] // FF
    route_weight = jnp.sum(jnp.where(expert_ids == own_expert, gate_pair, 0.0), axis=1)
    gate_part = jnp.dot(normed, w_gate, preferred_element_type=jnp.float32)
    up_projection_share = jnp.dot(normed, w_up, preferred_element_type=jnp.float32)
    hidden = (jax.nn.silu(gate_part) * up_projection_share).astype(jnp.bfloat16)
    term = lax.dot_general(
        expert_down_weight, hidden, (((0,), (1,)), ((), ())), preferred_element_type=jnp.float32
    )
    moe_rows = lax.psum_scatter(
        term * route_weight[None, :], "seq", scatter_dimension=0, tiled=True
    )
    stream_own = lax.dynamic_slice_in_dim(stream, out_start, out_width, 1)
    layer_out = (stream_own + moe_rows.T).astype(jnp.bfloat16)
    return (attn_proj, layer_out)


def solution(mesh):
    placed = (
        P("groups", None),
        P("groups", None),
        P("groups", None),
        P("groups", "seq", None),
        P("groups", "seq", None),
        P("groups"),
        P("groups", None),
        P("seq", None),
        P(),
        P(),
        P(None, "seq"),
        P(None, "seq"),
        P("seq", None),
        P("groups", None),
    )
    return jax.shard_map(
        per_device,
        mesh=mesh,
        in_specs=placed,
        out_specs=(P("groups", "seq"), P("groups", "seq")),
        check_vma=False,
    )
```

profile of v0, /device:TPU:0, one launch (start us, length us, event | category | flops | bytes accessed | tf_op | source)
XLA Modules:
  0.0 263.8 jit_solution(7450599788652511796)
XLA Ops:
  8.1 2.0 fusion.38
  10.1 1.7 fusion.7
  13.1 24.1 %all-gather.1 = f32[128,8,4]{1,2,0:T(4,128)S(1)} all-gather(f32[8,8,4]{1,2,0:T(4,128)S(1)} %copy.49), channel_id=3, replica_groups=mesh['groups'=2,'seq'=16] {'seq'}, dimensions={0}, use_global_device_ids=true | all-gather | bytes 17408 | tf_op jit(solution)/shard_map/all_gather | solution.py:15
  37.2 18.7 %all-gather = f32[128,8,4]{1,2,0:T(4,128)S(1)} all-gather(f32[8,8,4]{1,2,0:T(4,128)S(1)} %copy.48), channel_id=2, replica_groups=mesh['groups'=2,'seq'=16] {'seq'}, dimensions={0}, use_global_device_ids=true | all-gather | bytes 17408 | tf_op jit(solution)/shard_map/all_gather | solution.py:15
  56.0 1.0 fusion.23
  57.9 0.9 slice.40
  58.9 3.0 %slice.43 = f32[120,8,4,128]{3,1,2,0:T(8,128)} slice(f32[128,8,4,128]{3,1,2,0:T(8,128)} %all-gather.5.cloned.1.call-done), slice={[8:128], [0:8], [0:4], [0:128]} | slice | bytes 3932160 | tf_op jit(solution)/shard_map/slice | solution.py:17
  61.9 24.5 %while.14 = (s32[]{:T(128)}, f32[8,8,4]{1,2,0:T(4,128)S(1)}, f32[8,8,4]{1,2,0:T(4,128)S(1)}, f32[8,8,4,128]{3,2,1,0:T(4,128)S(1)}, f32[15,8,8,4]{2,3,1,0:T(4,128...) while((s32[]{:T(128)}, f32[8,8,4]{1,2,0:T(4,128)S(1)}, ...), condition=%wide.region_3.4_spmd, body=%wide.region_2.3_spmd.sunk | while | flops 99842 | bytes 669797 | solution.py:18
  63.8 0.9 constant_dynamic-slice_fusion.2
  65.4 0.9 constant_dynamic-slice_fusion.2
  67.0 0.9 constant_dynamic-slice_fusion.2
  68.7 0.9 constant_dynamic-slice_fusion.2
  70.3 0.9 constant_dynamic-slice_fusion.2
  72.0 0.9 constant_dynamic-slice_fusion.2
  73.6 0.9 constant_dynamic-slice_fusion.2
  75.2 0.9 constant_dynamic-slice_fusion.2
  87.1 1.0 fusion.31
  88.3 87.4 %all-reduce.2.cloned.1.call-done = f32[8,4096]{1,0:T(8,128)} async-done(((f32[8,4096]{1,0:T(8,128)}), f32[8,4096]{1,0:T(8,128)}) %all-reduce.2.cloned.1.call-update) | async-done | bytes 131088 | tf_op jit(solution)/shard_map/psum | solution.py:94
  175.8 1.1 multiply_reduce_fusion
  177.1 7.2 %fusion.39 = f32[8,1792]{1,0:T(8,128)S(1)} fusion(bf16[8,4096]{1,0:T(8,128)(2,1)S(1)} %multiply_convert_fusion, bf16[4096,1792]{1,0:T(8,128)(2,1)} %param.26), kind=kOutput, calls=%fused_computation.67 | convolution fusion | flops 117440512 | bytes 14802944 | tf_op jit(solution)/shard_map/dot_general | solution.py:113
  184.3 14.3 %fusion.4 = f32[4096,8]{0,1:T(8,128)} fusion(bf16[1792,4096]{1,0:T(8,128)(2,1)} %param.28, bf16[8,4096]{1,0:T(8,128)(2,1)S(1)} %multiply_convert_fusion, bf16[4096,1792]{1,0:T(8,128)(2,1)} %param.27, f32[8]{0:T(128)S(1)} %fusion.32, f32[8,1792]{1,0:T(8,128)S(1)} %fusion.39), kind=kOutput, calls=%fused_computation.11 | convolution fusion | flops 234999808 | bytes 29614112 | tf_op jit(solution)/shard_map/dot_general | solution.py:116
  198.6 1.3 dynamic-slice_convert_fusion
  199.9 56.0 %reduce-scatter.2.cloned.1.call-done = f32[256,8]{0,1:T(8,128)} async-done(((f32[4096,8]{0,1:T(8,128)}), f32[256,8]{0,1:T(8,128)}) %reduce-scatter.2.cloned.1.call-update) | async-done | bytes 8208 | tf_op jit(solution)/shard_map/reduce_scatter | solution.py:119
  255.9 1.3 fusion.30
  (111 shorter events, 21.2 us)
Async XLA Ops:
  7.2 80.0 %copy-start = (bf16[256,4096]{1,0:T(8,128)(2,1)S(1)}, bf16[256,4096]{1,0:T(8,128)(2,1)}, u32[]{:S(2)}) copy-start(bf16[256,4096]{1,0:T(8,128)(2,1)} %param.23) | copy-start | bytes 6291460
  7.2 81.1 %copy-start.2 = (bf16[4096]{0:T(1024)(128)(2,1)S(1)}, bf16[4096]{0:T(1024)(128)(2,1)}, u32[]{:S(2)}) copy-start(bf16[4096]{0:T(1024)(128)(2,1)} %param.24) | copy-start | bytes 24580
  7.2 168.6 %copy-start.1 = (bf16[8,4096]{1,0:T(8,128)(2,1)S(1)}, bf16[8,4096]{1,0:T(8,128)(2,1)}, u32[]{:S(2)}) copy-start(bf16[8,4096]{1,0:T(8,128)(2,1)} %param.22) | copy-start | bytes 196612
  7.2 169.7 %copy-start.4 = (bf16[4096,4]{0,1:T(4,128)(2,1)S(1)}, bf16[4096,4]{0,1:T(4,128)(2,1)}, u32[]{:S(2)}) copy-start(bf16[4096,4]{0,1:T(4,128)(2,1)} %param.25) | copy-start | bytes 98308
  7.2 169.9 %copy-start.3 = (s32[8,2]{0,1:T(2,128)S(1)}, s32[8,2]{0,1:T(2,128)}, u32[]{:S(2)}) copy-start(s32[8,2]{0,1:T(2,128)} %param.29) | copy-start | bytes 196
  7.2 50.7 %all-gather.5.cloned.1.call-start = ((), (), s32[]{:S(2)}) async-start(), calls=%async_computation.3 | async-start | bytes 2228224 | tf_op jit(solution)/shard_map/all_gather | solution.py:15
  12.5 163.2 %all-reduce.2.cloned.1.call-start = ((), (), s32[]{:S(2)}) async-start(), calls=%async_computation.1 | async-start | bytes 262144 | tf_op jit(solution)/shard_map/psum | solution.py:94
  88.2 167.7 %reduce-scatter.2.cloned.1.call-start = ((), (), s32[]{:S(2)}) async-start(), calls=%async_computation.2 | async-start | bytes 139264 | tf_op jit(solution)/shard_map/reduce_scatter | solution.py:119
Sparse Core Ops, SparseCore 0:
  12.6 44.5 all-gather.4
  88.3 87.3 all-reduce.1
  198.7 57.1 reduce-scatter.1
where the time goes:
time: 265 us; the launch traced here: 264 us
  waiting for transfers between devices  144 us (54%)
  blocking collectives  42.9 us (16%)
  matrix products  27.3 us (10%)
  local copies, waits for them, and re-layouts  24.1 us (9%)
  between operations  14 us (5%)
  other arithmetic  11.7 us (4%)
    psum x1, waiting for transfers between devices, per_device(): lax.psum(jnp.dot(context_own, w_out, preferred_element_type=jnp.float32),...  87.4 us
    reduce_scatter x1, waiting for transfers between devices, per_device(): lax.psum_scatter(term * route_weight[None, :], 'seq', scatter_dimension=0...  56 us
    all_gather x2, blocking collectives, joined(): pieces = jax.tree.map(lambda part: lax.all_gather(part, axis), value)  42.9 us
    dot_general x1, matrix products, per_device(): lax.dot_general(expert_down_weight, hidden, (((0,), (1,)), ((), ())), pre...  14.3 us
    dynamic_slice x15, local copies, waits for them, and re-layouts, joined(): lax.scan(lambda so_far, share: (join(so_far, share), None), head, tail)  13.7 us
    dot_general x1, matrix products, per_device(): gate_part = jnp.dot(normed, w_gate, preferred_element_type=jnp.float32)  7.18 us
    add x15, other arithmetic, merge_partial_results(): first_num * first_scale[..., None] + second_num * second_scale[..., None]  6.37 us
  transfers between devices with their start and end apart: 3, of which 2 were waited for; matrix products, arithmetic and copies ran while one was open for 1% of the time, Pallas kernels for 0%

commit v1 on v0

--- a/solution.py
+++ b/solution.py
@@ -91,7 +91,8 @@
     denominator = merged_sum * old_scale + fresh_weight
     context = (numerator / denominator[..., None]).reshape(flat_shape)
     context_own = lax.dynamic_slice_in_dim(context, feat_start, feat_width, 1).astype(jnp.bfloat16)
-    projected = lax.psum(jnp.dot(context_own, w_out, preferred_element_type=jnp.float32), "seq")
+    piece_in = jnp.dot(context_own, w_out, preferred_element_type=jnp.float32)
+    projected = lax.all_gather(piece_in, axis_name="seq").sum(axis=0)
     out_width = projected.shape[1] // lax.axis_size("seq")
     out_start = device * out_width
     attn_proj = lax.dynamic_slice_in_dim(projected, out_start, out_width, 1).astype(jnp.bfloat16)

time: 265 us -> 216 us (0.82)
  waiting for transfers between devices: 144 us -> 94.6 us
    psum x1 -> x0, waiting for transfers between devices: 87.4 us -> none  [per_device(): lax.psum(jnp.dot(context_own, w_out, preferred_element_type=jnp.float32),...]
    all_gather x0 -> x1, waiting for transfers between devices: none -> 40.6 us  [per_device(): projected = lax.all_gather(piece_in, axis_name='seq').sum(axis=0)]
where the time goes in v1:
time: 216 us; the launch traced here: 215 us
  waiting for transfers between devices  94.6 us (44%)
  blocking collectives  42.9 us (20%)
  matrix products  27.3 us (13%)
  local copies, waits for them, and re-layouts  23.4 us (11%)
  between operations  14 us (6%)
  other arithmetic  12.5 us (6%)
    reduce_scatter x1, waiting for transfers between devices, per_device(): lax.psum_scatter(term * route_weight[None, :], 'seq', scatter_dimension=0...  53.9 us
    all_gather x2, blocking collectives, joined(): pieces = jax.tree.map(lambda part: lax.all_gather(part, axis), value)  42.9 us
    all_gather x1, waiting for transfers between devices, per_device(): projected = lax.all_gather(piece_in, axis_name='seq').sum(axis=0)  40.6 us
    dot_general x1, matrix products, per_device(): lax.dot_general(expert_down_weight, hidden, (((0,), (1,)), ((), ())), pre...  14.2 us
    dynamic_slice x15, local copies, waits for them, and re-layouts, joined(): lax.scan(lambda so_far, share: (join(so_far, share), None), head, tail)  13.7 us
    dot_general x1, matrix products, per_device(): gate_part = jnp.dot(normed, w_gate, preferred_element_type=jnp.float32)  7.18 us
    add x15, other arithmetic, merge_partial_results(): first_num * first_scale[..., None] + second_num * second_scale[..., None]  6.37 us
  transfers between devices with their start and end apart: 3, of which 2 were waited for; matrix products, arithmetic and copies ran while one was open for 1% of the time, Pallas kernels for 0%

profile of v1, /device:TPU:0, one launch (start us, length us, event | category | flops | bytes accessed | tf_op | source)
XLA Modules:
  0.0 214.9 jit_solution(10120236217589581840)
XLA Ops:
  8.1 2.0 fusion.38
  10.1 1.7 fusion.7
  13.1 24.1 %all-gather.1 = f32[128,8,4]{1,2,0:T(4,128)S(1)} all-gather(f32[8,8,4]{1,2,0:T(4,128)S(1)} %copy.49), channel_id=3, replica_groups=mesh['groups'=2,'seq'=16] {'seq'}, dimensions={0}, use_global_device_ids=true | all-gather | bytes 17408 | tf_op jit(solution)/shard_map/all_gather | solution.py:15
  37.2 18.7 %all-gather = f32[128,8,4]{1,2,0:T(4,128)S(1)} all-gather(f32[8,8,4]{1,2,0:T(4,128)S(1)} %copy.48), channel_id=2, replica_groups=mesh['groups'=2,'seq'=16] {'seq'}, dimensions={0}, use_global_device_ids=true | all-gather | bytes 17408 | tf_op jit(solution)/shard_map/all_gather | solution.py:15
  56.0 1.0 fusion.23
  57.9 0.9 slice.40
  58.9 3.0 %slice.43 = f32[120,8,4,128]{3,1,2,0:T(8,128)} slice(f32[128,8,4,128]{3,1,2,0:T(8,128)} %all-gather.7.cloned.1.call-done), slice={[8:128], [0:8], [0:4], [0:128]} | slice | bytes 3932160 | tf_op jit(solution)/shard_map/slice | solution.py:17
  61.9 24.5 %while.14 = (s32[]{:T(128)}, f32[8,8,4]{1,2,0:T(4,128)S(1)}, f32[8,8,4]{1,2,0:T(4,128)S(1)}, f32[8,8,4,128]{3,2,1,0:T(4,128)S(1)}, f32[15,8,8,4]{2,3,1,0:T(4,128...) while((s32[]{:T(128)}, f32[8,8,4]{1,2,0:T(4,128)S(1)}, ...), condition=%wide.region_3.4_spmd, body=%wide.region_2.3_spmd.sunk | while | flops 99842 | bytes 669797 | solution.py:18
  63.8 0.9 constant_dynamic-slice_fusion.2
  65.4 0.9 constant_dynamic-slice_fusion.2
  67.0 0.9 constant_dynamic-slice_fusion.2
  68.7 0.9 constant_dynamic-slice_fusion.2
  70.3 0.9 constant_dynamic-slice_fusion.2
  72.0 0.9 constant_dynamic-slice_fusion.2
  73.6 0.9 constant_dynamic-slice_fusion.2
  75.2 0.9 constant_dynamic-slice_fusion.2
  76.9 0.9 constant_dynamic-slice_fusion.2
  87.1 1.0 fusion.31
  88.3 40.6 %all-gather.9.cloned.1.call-done = f32[128,4096]{1,0:T(8,128)} async-done(((f32[8,4096]{1,0:T(8,128)}), f32[128,4096]{1,0:T(8,128)}) %all-gather.9.cloned.1.call-update) | async-done | bytes 2097168 | tf_op jit(solution)/shard_map/all_gather | solution.py:95
  128.9 1.7 bitcast_reduce_fusion
  131.0 7.2 %fusion.39 = f32[8,1792]{1,0:T(8,128)S(1)} fusion(bf16[8,4096]{1,0:T(8,128)(2,1)S(1)} %multiply_convert_fusion, bf16[4096,1792]{1,0:T(8,128)(2,1)} %param.26), kind=kOutput, calls=%fused_computation.68 | convolution fusion | flops 117440512 | bytes 14802944 | tf_op jit(solution)/shard_map/dot_general | solution.py:114
  138.2 14.2 %fusion.4 = f32[4096,8]{0,1:T(8,128)} fusion(bf16[1792,4096]{1,0:T(8,128)(2,1)} %param.28, bf16[8,4096]{1,0:T(8,128)(2,1)S(1)} %multiply_convert_fusion, bf16[4096,1792]{1,0:T(8,128)(2,1)} %param.27, f32[8]{0:T(128)S(1)} %fusion.32, f32[8,1792]{1,0:T(8,128)S(1)} %fusion.39), kind=kOutput, calls=%fused_computation.11 | convolution fusion | flops 234999808 | bytes 29614112 | tf_op jit(solution)/shard_map/dot_general | solution.py:117
  153.1 53.9 %reduce-scatter.2.cloned.1.call-done = f32[256,8]{0,1:T(8,128)} async-done(((f32[4096,8]{0,1:T(8,128)}), f32[256,8]{0,1:T(8,128)}) %reduce-scatter.2.cloned.1.call-update) | async-done | bytes 8208 | tf_op jit(solution)/shard_map/reduce_scatter | solution.py:120
  207.1 1.3 fusion.30
  (112 shorter events, 21.1 us)
Async XLA Ops:
  7.2 80.0 %copy-start = (bf16[256,4096]{1,0:T(8,128)(2,1)S(1)}, bf16[256,4096]{1,0:T(8,128)(2,1)}, u32[]{:S(2)}) copy-start(bf16[256,4096]{1,0:T(8,128)(2,1)} %param.23) | copy-start | bytes 6291460
  7.2 81.1 %copy-start.2 = (bf16[4096]{0:T(1024)(128)(2,1)S(1)}, bf16[4096]{0:T(1024)(128)(2,1)}, u32[]{:S(2)}) copy-start(bf16[4096]{0:T(1024)(128)(2,1)} %param.24) | copy-start | bytes 24580
  7.2 123.4 %copy-start.1 = (bf16[8,4096]{1,0:T(8,128)(2,1)S(1)}, bf16[8,4096]{1,0:T(8,128)(2,1)}, u32[]{:S(2)}) copy-start(bf16[8,4096]{1,0:T(8,128)(2,1)} %param.22) | copy-start | bytes 196612
  7.2 123.6 %copy-start.4 = (bf16[4096,4]{0,1:T(4,128)(2,1)S(1)}, bf16[4096,4]{0,1:T(4,128)(2,1)}, u32[]{:S(2)}) copy-start(bf16[4096,4]{0,1:T(4,128)(2,1)} %param.25) | copy-start | bytes 98308
  7.2 123.8 %copy-start.3 = (s32[8,2]{0,1:T(2,128)S(1)}, s32[8,2]{0,1:T(2,128)}, u32[]{:S(2)}) copy-start(s32[8,2]{0,1:T(2,128)} %param.29) | copy-start | bytes 196
  7.2 50.7 %all-gather.7.cloned.1.call-start = ((), (), s32[]{:S(2)}) async-start(), calls=%async_computation.2 | async-start | bytes 2228224 | tf_op jit(solution)/shard_map/all_gather | solution.py:15
  12.5 116.4 %all-gather.9.cloned.1.call-start = ((), (), s32[]{:S(2)}) async-start(), calls=%async_computation.3 | async-start | bytes 2228224 | tf_op jit(solution)/shard_map/all_gather | solution.py:95
  88.2 118.9 %reduce-scatter.2.cloned.1.call-start = ((), (), s32[]{:S(2)}) async-start(), calls=%async_computation.1 | async-start | bytes 139264 | tf_op jit(solution)/shard_map/reduce_scatter | solution.py:120
Sparse Core Ops, SparseCore 0:
  12.6 44.5 all-gather.6
  88.3 40.4 all-gather.8
  152.6 54.3 reduce-scatter.1
